TPU v7x, 32 devices: a whole 2x2x4 slice. The times are simulated.
32 devices in a mesh: pipe: 4 (over x, core), exp: 4 (over z), pair: 2 (over y).
Axes of the slice: x: 2, y: 2, z: 4, core: 2. Of those that a mesh axis runs over, the one named last changes fastest.
Arguments:
- hidden_in: bfloat16 [4, 256, 2048], P(None, ('exp', 'pair')), may hold values from -6 to 6
- routes: int32 [4, 4, 256, 8], P('pipe', None, ('exp', 'pair')), may hold values from 0 to 15, all different within a row; in each aligned block of 32 rows (0 to 31, 32 to 63, ..., all dimensions but the last counted through in order) at most 24 rows name the same one
- gate_probs: float32 [4, 4, 256, 8], P('pipe', None, ('exp', 'pair')), may hold values from 0.02 to 1
- norm_gain: float32 [4, 2048], P('pipe'), may hold values from 0.1 to 1.9
- w_gate: bfloat16 [4, 16, 2048, 768], P('pipe', ('exp', 'pair')), may hold values from -0.125 to 0.125
- w_up: bfloat16 [4, 16, 2048, 768], P('pipe', ('exp', 'pair')), may hold values from -0.125 to 0.125
- w_down: bfloat16 [4, 16, 768, 2048], P('pipe', ('exp', 'pair')), may hold values from -0.21875 to 0.21875
Outputs:
- layer_outputs: bfloat16 [4, 4, 256, 2048], P('pipe', None, ('exp', 'pair'))
Inputs may be any that keep to these rules, and one draw needn't show every extreme that they name: `routes`: within each layer and micro-batch, the 32 tokens of one device (aligned blocks) name no expert more than 24 times in all, and each token names 8 different experts.
All inputs are finite; a program needn't handle non-finite values.
Results may differ from a plain program's by a relative error of at most 0.01.
Values may be sent and summed in bfloat16 or wider, within the bound.
A program may use at most 64 MiB of HBM per device.

v0:
```python
import jax
import jax.numpy as jnp
from jax import lax
from jax.sharding import PartitionSpec as P

EPS = 1e-06


def passed_along(value, axis, steps):
    count = lax.axis_size(axis)
    first, last = (max(0, -steps), min(count, count - steps))
    return lax.ppermute(value, axis, [(source, source + steps) for source in range(first, last)])


def expert_block(arrived, wgate, wupper, wdown):
    gate = jnp.einsum("nlcd,ldf->nlcf", arrived, wgate, preferred_element_type=jnp.float32)
    upward = jnp.einsum("nlcd,ldf->nlcf", arrived, wupper, preferred_element_type=jnp.float32)
    hidden = (jax.nn.silu(gate) * upward).astype(jnp.bfloat16)
    return jnp.einsum("nlcf,lfd->nlcd", hidden, wdown, preferred_element_type=jnp.float32).astype(
        jnp.bfloat16
    )


def on_device(hidden_in, routes, gate_probs, norm_gain, w_gate, w_up, w_down):
    section = lax.axis_index("pipe")
    micro, tok_rows, width = hidden_in.shape
    top_count = routes.shape[3]
    groups = lax.axis_size(("exp", "pair"))
    local_experts = w_gate.shape[1]
    experts = local_experts * groups
    capacity = max(2, 3 * tok_rows * top_count // (2 * experts))
    gain = norm_gain[0]
    wgate = w_gate[0]
    wupper = w_up[0]
    wdown = w_down[0]
    expert_ids = jnp.arange(experts, dtype=jnp.int32)

    def layer(state, index):
        chosen = lax.dynamic_index_in_dim(routes[0], index, 0, keepdims=False).reshape(-1)
        probs = lax.dynamic_index_in_dim(gate_probs[0], index, 0, keepdims=False)
        floated = state.astype(jnp.float32)
        scale = lax.rsqrt(jnp.mean(floated * floated, axis=-1, keepdims=True) + EPS)
        normed = (floated * scale * gain).astype(jnp.bfloat16)
        onehot = (chosen[:, None] == expert_ids[None, :]).astype(jnp.int32)
        before = jnp.cumsum(onehot, axis=0) - onehot
        slots = jnp.sum(before * onehot, axis=1)
        outgoing = jnp.zeros((experts, capacity, width), jnp.bfloat16)
        outgoing = outgoing.at[chosen, slots].set(jnp.repeat(normed, top_count, axis=0))
        grouped = outgoing.reshape(groups, local_experts, capacity, width)
        produced = expert_block(
            lax.all_to_all(grouped, ("exp", "pair"), split_axis=0, concat_axis=0, tiled=True),
            wgate,
            wupper,
            wdown,
        )
        returned = lax.all_to_all(
            produced, ("exp", "pair"), split_axis=0, concat_axis=0, tiled=True
        )
        results = returned.reshape(experts, capacity, width)[chosen, slots]
        results = results.reshape(tok_rows, top_count, width).astype(jnp.float32)
        weights = probs / jnp.sum(probs, axis=-1, keepdims=True)
        mixed = jnp.einsum("tk,tkd->td", weights, results)
        return (floated + mixed).astype(jnp.bfloat16)

    def advance(step, carry):
        received, saved = carry
        index = step - section
        valid = jnp.logical_and(index >= 0, index < micro)
        clipped = jnp.clip(index, 0, micro - 1)
        first = lax.dynamic_index_in_dim(hidden_in, clipped, 0, keepdims=False)
        state = jnp.where(section == 0, first, received)
        updated = layer(state, clipped)
        saved = jnp.where(valid, lax.dynamic_update_index_in_dim(saved, updated, clipped, 0), saved)
        received = passed_along(updated, "pipe", 1)
        return (received, saved)

    start = (
        jnp.zeros((tok_rows, width), jnp.bfloat16),
        jnp.zeros((micro, tok_rows, width), jnp.bfloat16),
    )
    received, saved = lax.fori_loop(0, micro + lax.axis_size("pipe") - 1, advance, start)
    return saved[None]


def solution(mesh):
    in_specs = (
        P(None, ("exp", "pair"), None),
        P("pipe", None, ("exp", "pair"), None),
        P("pipe", None, ("exp", "pair"), None),
        P("pipe", None),
        P("pipe", ("exp", "pair"), None, None),
        P("pipe", ("exp", "pair"), None, None),
        P("pipe", ("exp", "pair"), None, None),
    )
    out_specs = P("pipe", None, ("exp", "pair"), None)
    return jax.shard_map(
        on_device, mesh=mesh, in_specs=in_specs, out_specs=out_specs, check_vma=False
    )
```

profile of v0, /device:TPU:1, one launch (start us, length us, event | category | flops | bytes accessed | tf_op | source)
XLA Modules:
  0.0 937.2 jit_solution(15736673222117613759)
XLA Ops:
  0.9 936.4 %while.18 = (s32[]{:T(128)}, bf16[32,2048]{1,0:T(8,128)(2,1)S(1)}, bf16[4,32,2048]{2,1,0:T(8,128)(2,1)}, pred[]{:T(512)}, s32[]{:T(128)}, /*index=5*/bf16[4,32,2...) while((s32[]{:T(128)}, bf16[32,2048]{1,0:T(8,128)(2,1)S(1)}, ...), condition=%wide.region_7.8_spmd.clone.clone, body=%wide.region_0.7_spmd.clone.clone.sunk | while | flops 3628826880 | bytes 48352280 | solution.py:81
  5.1 23.0 %scatter_fusion = bf16[16,24,2048]{2,1,0:T(8,128)(2,1)S(1)} fusion(bf16[16,24,2048]{2,1,0:T(8,128)(2,1)S(1)} %broadcast.269, s32[256]{0:T(256)S(1)} %bitcast.143, bf16[256,2048]{1,0:T(8,128)(2,1)S(1)} %broadcast_bitcast_fusion.2), kind=kCustom, calls=%fused_computation.1.clone.clone.1 | custom fusion | bytes 3147776 | tf_op jit(solution)/shard_map/while/body/eval_jaxpr/scatter | solution.py:48
  28.1 42.3 %all_to_all.26 = bf16[8,2,24,2048]{3,2,1,0:T(8,128)(2,1)S(1)} all-to-all(bf16[8,2,24,2048]{3,2,1,0:T(8,128)(2,1)S(1)} %bitcast.140), channel_id=1, replica_groups=mesh['pipe'=4,'exp'=4,'pair'=2] {'exp','pair'}, dimensions={0} | all-to-all | bytes 3145728 | tf_op jit(solution)/shard_map/while/body/eval_jaxpr/all_to_all | solution.py:51
  70.4 5.2 fusion.86
  75.6 8.0 fusion.87
  84.8 4.3 all-to-all-start.1
  89.2 35.8 %all-to-all-done.1 = bf16[8,2,24,2048]{3,2,1,0:T(8,128)(2,1)S(1)} async-done(((bf16[8,2,24,2048]{3,2,1,0:T(8,128)(2,1)}), bf16[8,2,24,2048]{3,2,1,0:T(8,128)(2,1)S(1)}, u32[]{:S(2)}, u32[]{:S(2)}) %all-to-all-start.1) | async-done | bytes 1572896 | tf_op jit(solution)/shard_map/while/body/eval_jaxpr/all_to_all | solution.py:56
  125.0 4.3 gather_fusion
  131.5 4.7 collective-permute-start
  136.1 1.9 collective-permute-done
  142.3 23.0 %scatter_fusion = bf16[16,24,2048]{2,1,0:T(8,128)(2,1)S(1)} fusion(bf16[16,24,2048]{2,1,0:T(8,128)(2,1)S(1)} %broadcast.269, s32[256]{0:T(256)S(1)} %bitcast.143, bf16[256,2048]{1,0:T(8,128)(2,1)S(1)} %broadcast_bitcast_fusion.2), kind=kCustom, calls=%fused_computation.1.clone.clone.1 | custom fusion | bytes 3147776 | tf_op jit(solution)/shard_map/while/body/eval_jaxpr/scatter | solution.py:48
  165.3 39.4 %all_to_all.26 = bf16[8,2,24,2048]{3,2,1,0:T(8,128)(2,1)S(1)} all-to-all(bf16[8,2,24,2048]{3,2,1,0:T(8,128)(2,1)S(1)} %bitcast.140), channel_id=1, replica_groups=mesh['pipe'=4,'exp'=4,'pair'=2] {'exp','pair'}, dimensions={0} | all-to-all | bytes 3145728 | tf_op jit(solution)/shard_map/while/body/eval_jaxpr/all_to_all | solution.py:51
  204.7 5.2 fusion.86
  209.9 8.0 fusion.87
  219.1 3.7 all-to-all-start.1
  223.0 36.4 %all-to-all-done.1 = bf16[8,2,24,2048]{3,2,1,0:T(8,128)(2,1)S(1)} async-done(((bf16[8,2,24,2048]{3,2,1,0:T(8,128)(2,1)}), bf16[8,2,24,2048]{3,2,1,0:T(8,128)(2,1)S(1)}, u32[]{:S(2)}, u32[]{:S(2)}) %all-to-all-start.1) | async-done | bytes 1572896 | tf_op jit(solution)/shard_map/while/body/eval_jaxpr/all_to_all | solution.py:56
  259.4 4.3 gather_fusion
  265.8 2.2 collective-permute-start
  268.0 1.9 collective-permute-done
  274.1 23.0 %scatter_fusion = bf16[16,24,2048]{2,1,0:T(8,128)(2,1)S(1)} fusion(bf16[16,24,2048]{2,1,0:T(8,128)(2,1)S(1)} %broadcast.269, s32[256]{0:T(256)S(1)} %bitcast.143, bf16[256,2048]{1,0:T(8,128)(2,1)S(1)} %broadcast_bitcast_fusion.2), kind=kCustom, calls=%fused_computation.1.clone.clone.1 | custom fusion | bytes 3147776 | tf_op jit(solution)/shard_map/while/body/eval_jaxpr/scatter | solution.py:48
  297.1 41.0 %all_to_all.26 = bf16[8,2,24,2048]{3,2,1,0:T(8,128)(2,1)S(1)} all-to-all(bf16[8,2,24,2048]{3,2,1,0:T(8,128)(2,1)S(1)} %bitcast.140), channel_id=1, replica_groups=mesh['pipe'=4,'exp'=4,'pair'=2] {'exp','pair'}, dimensions={0} | all-to-all | bytes 3145728 | tf_op jit(solution)/shard_map/while/body/eval_jaxpr/all_to_all | solution.py:51
  338.1 5.2 fusion.86
  343.3 8.0 fusion.87
  352.5 3.8 all-to-all-start.1
  356.5 36.3 %all-to-all-done.1 = bf16[8,2,24,2048]{3,2,1,0:T(8,128)(2,1)S(1)} async-done(((bf16[8,2,24,2048]{3,2,1,0:T(8,128)(2,1)}), bf16[8,2,24,2048]{3,2,1,0:T(8,128)(2,1)S(1)}, u32[]{:S(2)}, u32[]{:S(2)}) %all-to-all-start.1) | async-done | bytes 1572896 | tf_op jit(solution)/shard_map/while/body/eval_jaxpr/all_to_all | solution.py:56
  392.8 4.3 gather_fusion
  399.2 1.9 collective-permute-start
  401.1 1.9 collective-permute-done
  407.2 23.0 %scatter_fusion = bf16[16,24,2048]{2,1,0:T(8,128)(2,1)S(1)} fusion(bf16[16,24,2048]{2,1,0:T(8,128)(2,1)S(1)} %broadcast.269, s32[256]{0:T(256)S(1)} %bitcast.143, bf16[256,2048]{1,0:T(8,128)(2,1)S(1)} %broadcast_bitcast_fusion.2), kind=kCustom, calls=%fused_computation.1.clone.clone.1 | custom fusion | bytes 3147776 | tf_op jit(solution)/shard_map/while/body/eval_jaxpr/scatter | solution.py:48
  430.2 41.4 %all_to_all.26 = bf16[8,2,24,2048]{3,2,1,0:T(8,128)(2,1)S(1)} all-to-all(bf16[8,2,24,2048]{3,2,1,0:T(8,128)(2,1)S(1)} %bitcast.140), channel_id=1, replica_groups=mesh['pipe'=4,'exp'=4,'pair'=2] {'exp','pair'}, dimensions={0} | all-to-all | bytes 3145728 | tf_op jit(solution)/shard_map/while/body/eval_jaxpr/all_to_all | solution.py:51
  471.7 5.2 fusion.86
  476.9 8.0 fusion.87
  486.1 3.7 all-to-all-start.1
  490.0 36.1 %all-to-all-done.1 = bf16[8,2,24,2048]{3,2,1,0:T(8,128)(2,1)S(1)} async-done(((bf16[8,2,24,2048]{3,2,1,0:T(8,128)(2,1)}), bf16[8,2,24,2048]{3,2,1,0:T(8,128)(2,1)S(1)}, u32[]{:S(2)}, u32[]{:S(2)}) %all-to-all-start.1) | async-done | bytes 1572896 | tf_op jit(solution)/shard_map/while/body/eval_jaxpr/all_to_all | solution.py:56
  526.0 4.3 gather_fusion
  532.5 1.9 collective-permute-start
  534.4 1.9 collective-permute-done
  540.5 23.0 %scatter_fusion = bf16[16,24,2048]{2,1,0:T(8,128)(2,1)S(1)} fusion(bf16[16,24,2048]{2,1,0:T(8,128)(2,1)S(1)} %broadcast.269, s32[256]{0:T(256)S(1)} %bitcast.143, bf16[256,2048]{1,0:T(8,128)(2,1)S(1)} %broadcast_bitcast_fusion.2), kind=kCustom, calls=%fused_computation.1.clone.clone.1 | custom fusion | bytes 3147776 | tf_op jit(solution)/shard_map/while/body/eval_jaxpr/scatter | solution.py:48
  563.5 41.6 %all_to_all.26 = bf16[8,2,24,2048]{3,2,1,0:T(8,128)(2,1)S(1)} all-to-all(bf16[8,2,24,2048]{3,2,1,0:T(8,128)(2,1)S(1)} %bitcast.140), channel_id=1, replica_groups=mesh['pipe'=4,'exp'=4,'pair'=2] {'exp','pair'}, dimensions={0} | all-to-all | bytes 3145728 | tf_op jit(solution)/shard_map/while/body/eval_jaxpr/all_to_all | solution.py:51
  605.1 5.2 fusion.86
  610.3 8.0 fusion.87
  619.5 3.8 all-to-all-start.1
  623.5 36.3 %all-to-all-done.1 = bf16[8,2,24,2048]{3,2,1,0:T(8,128)(2,1)S(1)} async-done(((bf16[8,2,24,2048]{3,2,1,0:T(8,128)(2,1)}), bf16[8,2,24,2048]{3,2,1,0:T(8,128)(2,1)S(1)}, u32[]{:S(2)}, u32[]{:S(2)}) %all-to-all-start.1) | async-done | bytes 1572896 | tf_op jit(solution)/shard_map/while/body/eval_jaxpr/all_to_all | solution.py:56
  659.8 4.3 gather_fusion
  666.2 1.9 collective-permute-start
  668.1 1.9 collective-permute-done
  674.2 23.0 %scatter_fusion = bf16[16,24,2048]{2,1,0:T(8,128)(2,1)S(1)} fusion(bf16[16,24,2048]{2,1,0:T(8,128)(2,1)S(1)} %broadcast.269, s32[256]{0:T(256)S(1)} %bitcast.143, bf16[256,2048]{1,0:T(8,128)(2,1)S(1)} %broadcast_bitcast_fusion.2), kind=kCustom, calls=%fused_computation.1.clone.clone.1 | custom fusion | bytes 3147776 | tf_op jit(solution)/shard_map/while/body/eval_jaxpr/scatter | solution.py:48
  697.3 41.4 %all_to_all.26 = bf16[8,2,24,2048]{3,2,1,0:T(8,128)(2,1)S(1)} all-to-all(bf16[8,2,24,2048]{3,2,1,0:T(8,128)(2,1)S(1)} %bitcast.140), channel_id=1, replica_groups=mesh['pipe'=4,'exp'=4,'pair'=2] {'exp','pair'}, dimensions={0} | all-to-all | bytes 3145728 | tf_op jit(solution)/shard_map/while/body/eval_jaxpr/all_to_all | solution.py:51
  738.7 5.2 fusion.86
  743.9 8.0 fusion.87
  753.1 3.8 all-to-all-start.1
  757.1 36.3 %all-to-all-done.1 = bf16[8,2,24,2048]{3,2,1,0:T(8,128)(2,1)S(1)} async-done(((bf16[8,2,24,2048]{3,2,1,0:T(8,128)(2,1)}), bf16[8,2,24,2048]{3,2,1,0:T(8,128)(2,1)S(1)}, u32[]{:S(2)}, u32[]{:S(2)}) %all-to-all-start.1) | async-done | bytes 1572896 | tf_op jit(solution)/shard_map/while/body/eval_jaxpr/all_to_all | solution.py:56
  793.4 4.3 gather_fusion
  799.8 1.9 collective-permute-start
  801.7 1.9 collective-permute-done
  807.8 23.0 %scatter_fusion = bf16[16,24,2048]{2,1,0:T(8,128)(2,1)S(1)} fusion(bf16[16,24,2048]{2,1,0:T(8,128)(2,1)S(1)} %broadcast.269, s32[256]{0:T(256)S(1)} %bitcast.143, bf16[256,2048]{1,0:T(8,128)(2,1)S(1)} %broadcast_bitcast_fusion.2), kind=kCustom, calls=%fused_computation.1.clone.clone.1 | custom fusion | bytes 3147776 | tf_op jit(solution)/shard_map/while/body/eval_jaxpr/scatter | solution.py:48
  830.8 41.4 %all_to_all.26 = bf16[8,2,24,2048]{3,2,1,0:T(8,128)(2,1)S(1)} all-to-all(bf16[8,2,24,2048]{3,2,1,0:T(8,128)(2,1)S(1)} %bitcast.140), channel_id=1, replica_groups=mesh['pipe'=4,'exp'=4,'pair'=2] {'exp','pair'}, dimensions={0} | all-to-all | bytes 3145728 | tf_op jit(solution)/shard_map/while/body/eval_jaxpr/all_to_all | solution.py:51
  872.3 5.2 fusion.86
  877.5 8.0 fusion.87
  886.7 3.8 all-to-all-start.1
  890.6 36.3 %all-to-all-done.1 = bf16[8,2,24,2048]{3,2,1,0:T(8,128)(2,1)S(1)} async-done(((bf16[8,2,24,2048]{3,2,1,0:T(8,128)(2,1)}), bf16[8,2,24,2048]{3,2,1,0:T(8,128)(2,1)S(1)}, u32[]{:S(2)}, u32[]{:S(2)}) %all-to-all-start.1) | async-done | bytes 1572896 | tf_op jit(solution)/shard_map/while/body/eval_jaxpr/all_to_all | solution.py:56
  926.9 4.3 gather_fusion
  933.4 1.9 collective-permute-start
  935.3 1.9 collective-permute-done
  (177 shorter events, 54.3 us)
Async XLA Ops:
  84.8 4.3 copy-start
  84.8 40.2 %all-to-all-start.1 = ((bf16[8,2,24,2048]{3,2,1,0:T(8,128)(2,1)}), bf16[8,2,24,2048]{3,2,1,0:T(8,128)(2,1)S(1)}, u32[]{:S(2)}, u32[]{:S(2)}) async-start(bf16[8,2,24,2048]{3,2,1,0:T(8,128)(2,1)} %copy.47), calls=%async_computation.1 | async-start | bytes 3145728 | tf_op jit(solution)/shard_map/while/body/eval_jaxpr/all_to_all | solution.py:56
  131.5 6.6 collective-permute-start
  219.1 3.7 copy-start
  219.1 40.2 %all-to-all-start.1 = ((bf16[8,2,24,2048]{3,2,1,0:T(8,128)(2,1)}), bf16[8,2,24,2048]{3,2,1,0:T(8,128)(2,1)S(1)}, u32[]{:S(2)}, u32[]{:S(2)}) async-start(bf16[8,2,24,2048]{3,2,1,0:T(8,128)(2,1)} %copy.47), calls=%async_computation.1 | async-start | bytes 3145728 | tf_op jit(solution)/shard_map/while/body/eval_jaxpr/all_to_all | solution.py:56
  265.8 4.1 collective-permute-start
  352.5 3.8 copy-start
  352.5 40.2 %all-to-all-start.1 = ((bf16[8,2,24,2048]{3,2,1,0:T(8,128)(2,1)}), bf16[8,2,24,2048]{3,2,1,0:T(8,128)(2,1)S(1)}, u32[]{:S(2)}, u32[]{:S(2)}) async-start(bf16[8,2,24,2048]{3,2,1,0:T(8,128)(2,1)} %copy.47), calls=%async_computation.1 | async-start | bytes 3145728 | tf_op jit(solution)/shard_map/while/body/eval_jaxpr/all_to_all | solution.py:56
  399.2 3.8 collective-permute-start
  486.1 3.7 copy-start
  486.1 39.9 %all-to-all-start.1 = ((bf16[8,2,24,2048]{3,2,1,0:T(8,128)(2,1)}), bf16[8,2,24,2048]{3,2,1,0:T(8,128)(2,1)S(1)}, u32[]{:S(2)}, u32[]{:S(2)}) async-start(bf16[8,2,24,2048]{3,2,1,0:T(8,128)(2,1)} %copy.47), calls=%async_computation.1 | async-start | bytes 3145728 | tf_op jit(solution)/shard_map/while/body/eval_jaxpr/all_to_all | solution.py:56
  532.5 3.8 collective-permute-start
  619.5 3.8 copy-start
  619.5 40.2 %all-to-all-start.1 = ((bf16[8,2,24,2048]{3,2,1,0:T(8,128)(2,1)}), bf16[8,2,24,2048]{3,2,1,0:T(8,128)(2,1)S(1)}, u32[]{:S(2)}, u32[]{:S(2)}) async-start(bf16[8,2,24,2048]{3,2,1,0:T(8,128)(2,1)} %copy.47), calls=%async_computation.1 | async-start | bytes 3145728 | tf_op jit(solution)/shard_map/while/body/eval_jaxpr/all_to_all | solution.py:56
  666.2 3.8 collective-permute-start
  753.1 3.8 copy-start
  753.1 40.2 %all-to-all-start.1 = ((bf16[8,2,24,2048]{3,2,1,0:T(8,128)(2,1)}), bf16[8,2,24,2048]{3,2,1,0:T(8,128)(2,1)S(1)}, u32[]{:S(2)}, u32[]{:S(2)}) async-start(bf16[8,2,24,2048]{3,2,1,0:T(8,128)(2,1)} %copy.47), calls=%async_computation.1 | async-start | bytes 3145728 | tf_op jit(solution)/shard_map/while/body/eval_jaxpr/all_to_all | solution.py:56
  799.8 3.8 collective-permute-start
  886.7 3.8 copy-start
  886.7 40.2 %all-to-all-start.1 = ((bf16[8,2,24,2048]{3,2,1,0:T(8,128)(2,1)}), bf16[8,2,24,2048]{3,2,1,0:T(8,128)(2,1)S(1)}, u32[]{:S(2)}, u32[]{:S(2)}) async-start(bf16[8,2,24,2048]{3,2,1,0:T(8,128)(2,1)} %copy.47), calls=%async_computation.1 | async-start | bytes 3145728 | tf_op jit(solution)/shard_map/while/body/eval_jaxpr/all_to_all | solution.py:56
  933.4 3.8 collective-permute-start
where the time goes:
time: 940 us; the launch traced here: 937 us
  blocking collectives  289 us (31%)
  waiting for transfers between devices  267 us (28%)
  local copies, waits for them, and re-layouts  212 us (23%)
  matrix products  95.1 us (10%)
  starting transfers between devices  43.2 us (5%)
  other arithmetic  30.3 us (3%)
    all_to_all x7, blocking collectives, layer(): lax.all_to_all(grouped, ('exp', 'pair'), split_axis=0, concat_axis=0, til...  289 us
    all_to_all x7, waiting for transfers between devices, layer(): lax.all_to_all(produced, ('exp', 'pair'), split_axis=0, concat_axis=0, ti...  253 us
    scatter x7, local copies, waits for them, and re-layouts, layer(): outgoing.at[chosen, slots].set(jnp.repeat(normed, top_count, axis=0))  161 us
    dot_general x7, matrix products, expert_block(): jnp.einsum('nlcf,lfd->nlcd', hidden, wdown, preferred_element_type=jnp.fl...  55.9 us
    dot_general x7, matrix products, expert_block(): jnp.einsum('nlcd,ldf->nlcf', arrived, wgate, preferred_element_type=jnp.f...  36.3 us
    gather x7, local copies, waits for them, and re-layouts, layer(): results = returned.reshape(experts, capacity, width)[chosen, slots]  30.3 us
    all_to_all x7, starting transfers between devices, layer(): lax.all_to_all(produced, ('exp', 'pair'), split_axis=0, concat_axis=0, ti...  26.8 us
  transfers between devices with their start and end apart: 14, of which 14 were waited for; matrix products, arithmetic and copies ran while one was open for 0% of the time, Pallas kernels for 0%

commit v1 on v0

--- a/solution.py
+++ b/solution.py
@@ -4,6 +4,29 @@
 from jax.sharding import PartitionSpec as P
 
 EPS = 1e-06
+
+
+def split_up(x, dim, length):
+    before, after = (x.shape[:dim], x.shape[dim + 1 :])
+    return jnp.moveaxis(x.reshape(*before, length, -1, *after), dim, 0)
+
+
+def joined_along(tiles, dim):
+    tiles = jnp.moveaxis(tiles, 0, dim)
+    shape = tiles.shape
+    return tiles.reshape(*shape[:dim], shape[dim] * shape[dim + 1], *shape[dim + 2 :])
+
+
+def exchange_directly(x, axis, split_dim, concat_dim):
+    count, mine = (lax.axis_size(axis), lax.axis_index(axis))
+    pieces = split_up(x, split_dim, count)
+    out = pieces
+    for step in range(1, count):
+        target, source = ((mine + step) % count, (mine - step) % count)
+        sent = lax.dynamic_index_in_dim(pieces, target, 0)
+        received = lax.ppermute(sent, axis, [(i, (i + step) % count) for i in range(count)])
+        out = lax.dynamic_update_slice_in_dim(out, received, source, axis=0)
+    return joined_along(out, concat_dim)
 
 
 def passed_along(value, axis, steps):
@@ -48,10 +71,7 @@
         outgoing = outgoing.at[chosen, slots].set(jnp.repeat(normed, top_count, axis=0))
         grouped = outgoing.reshape(groups, local_experts, capacity, width)
         produced = expert_block(
-            lax.all_to_all(grouped, ("exp", "pair"), split_axis=0, concat_axis=0, tiled=True),
-            wgate,
-            wupper,
-            wdown,
+            exchange_directly(grouped, ("exp", "pair"), 0, 0), wgate, wupper, wdown
         )
         returned = lax.all_to_all(
             produced, ("exp", "pair"), split_axis=0, concat_axis=0, tiled=True

time: 940 us -> 923 us (0.982)
  blocking collectives: 289 us -> 0 us
  starting transfers between devices: 43.2 us -> 202 us
  waiting for transfers between devices: 267 us -> 358 us
  local copies, waits for them, and re-layouts: 212 us -> 234 us
    all_to_all x7 -> x0, blocking collectives: 289 us -> none  [layer(): lax.all_to_all(grouped, ('exp', 'pair'), split_axis=0, concat_axis=0, til...]
    ppermute x0 -> x49, waiting for transfers between devices: none -> 91.7 us  [exchange_directly(): lax.ppermute(sent, axis, [(i, (i + step) % count) for i in range(count)])]
    all_to_all x7, starting transfers between devices: 26.8 us -> 102 us  [layer(): lax.all_to_all(produced, ('exp', 'pair'), split_axis=0, concat_axis=0, ti...]
    ppermute x0 -> x49, starting transfers between devices: none -> 74.1 us  [exchange_directly(): lax.ppermute(sent, axis, [(i, (i + step) % count) for i in range(count)])]
    dynamic_update_slice x0 -> x49, local copies, waits for them, and re-layouts: none -> 20.3 us  [exchange_directly(): out = lax.dynamic_update_slice_in_dim(out, received, source, axis=0)]
    ppermute x7, starting transfers between devices: 16.4 us -> 25.8 us  [passed_along(): lax.ppermute(value, axis, [(source, source + steps) for source in range(f...]
  transfers between devices with their start and end apart: 14 -> 63, of which waited for: 14 -> 28; matrix products, arithmetic and copies ran while one was open for 0% -> 2% of each run, Pallas kernels for 0% -> 0%
where the time goes in v1:
time: 923 us; the launch traced here: 921 us
  waiting for transfers between devices  358 us (39%)
  local copies, waits for them, and re-layouts  234 us (25%)
  starting transfers between devices  202 us (22%)
  matrix products  95.1 us (10%)
  other arithmetic  30.3 us (3%)
    all_to_all x7, waiting for transfers between devices, layer(): lax.all_to_all(produced, ('exp', 'pair'), split_axis=0, concat_axis=0, ti...  253 us
    scatter x7, local copies, waits for them, and re-layouts, layer(): outgoing.at[chosen, slots].set(jnp.repeat(normed, top_count, axis=0))  161 us
    all_to_all x7, starting transfers between devices, layer(): lax.all_to_all(produced, ('exp', 'pair'), split_axis=0, concat_axis=0, ti...  102 us
    ppermute x49, waiting for transfers between devices, exchange_directly(): lax.ppermute(sent, axis, [(i, (i + step) % count) for i in range(count)])  91.7 us
    ppermute x49, starting transfers between devices, exchange_directly(): lax.ppermute(sent, axis, [(i, (i + step) % count) for i in range(count)])  74.1 us
    dot_general x7, matrix products, expert_block(): jnp.einsum('nlcf,lfd->nlcd', hidden, wdown, preferred_element_type=jnp.fl...  55.9 us
    dot_general x7, matrix products, expert_block(): jnp.einsum('nlcd,ldf->nlcf', arrived, wgate, preferred_element_type=jnp.f...  36.3 us
    gather x7, local copies, waits for them, and re-layouts, layer(): results = returned.reshape(experts, capacity, width)[chosen, slots]  30.3 us
  transfers between devices with their start and end apart: 63, of which 28 were waited for; matrix products, arithmetic and copies ran while one was open for 2% of the time, Pallas kernels for 0%

profile of v1, /device:TPU:1, one launch (start us, length us, event | category | flops | bytes accessed | tf_op | source)
XLA Modules:
  0.0 920.6 jit_solution(4657717533576197523)
XLA Ops:
  0.9 919.7 %while.19 = (s32[]{:T(128)}, bf16[32,2048]{1,0:T(8,128)(2,1)S(1)}, bf16[4,32,2048]{2,1,0:T(8,128)(2,1)}, pred[]{:T(512)}, s32[]{:T(128)}, /*index=5*/bf16[4,32,2...) while((s32[]{:T(128)}, bf16[32,2048]{1,0:T(8,128)(2,1)S(1)}, ...), condition=%wide.region_7.8_spmd.clone.clone, body=%wide.region_0.7_spmd.clone.clone.sunk | while | flops 3628827136 | bytes 56219292 | solution.py:101
  5.2 23.0 %scatter_fusion = bf16[16,24,2048]{2,1,0:T(8,128)(2,1)S(1)} fusion(bf16[16,24,2048]{2,1,0:T(8,128)(2,1)S(1)} %broadcast.309, s32[256]{0:T(256)S(1)} %bitcast.171, bf16[256,2048]{1,0:T(8,128)(2,1)S(1)} %broadcast_bitcast_fusion.2), kind=kCustom, calls=%fused_computation.1.clone.clone.1 | custom fusion | bytes 3147776 | tf_op jit(solution)/shard_map/while/body/eval_jaxpr/scatter | solution.py:71
  44.5 11.4 %collective-permute-done.2 = bf16[1,1,2,24,2048]{4,3,2,1,0:T(8,128)(2,1)} collective-permute-done((bf16[1,1,2,24,2048]{4,3,2,1,0:T(8,128)(2,1)S(1)}, bf16[1,1,2,24,2048]{4,3,2,1,0:T(8,128)(2,1)}, u32[]{:S(2)}, u32[]{:S(2)}) %collective-permute-start.2) | collective-permute-done | bytes 196640 | tf_op jit(solution)/shard_map/while/body/eval_jaxpr/ppermute | solution.py:27
  57.0 5.2 fusion.80
  62.2 8.0 fusion.81
  71.5 14.3 %all-to-all-start = ((bf16[8,2,24,2048]{3,2,1,0:T(8,128)(2,1)}), bf16[8,2,24,2048]{3,2,1,0:T(8,128)(2,1)S(1)}, u32[]{:S(2)}, u32[]{:S(2)}) async-start(bf16[8,2,24,2048]{3,2,1,0:T(8,128)(2,1)} %copy.53), calls=%async_computation | async-start | bytes 3145728 | tf_op jit(solution)/shard_map/while/body/eval_jaxpr/all_to_all | solution.py:76
  85.9 35.0 %all-to-all-done = bf16[8,2,24,2048]{3,2,1,0:T(8,128)(2,1)S(1)} async-done(((bf16[8,2,24,2048]{3,2,1,0:T(8,128)(2,1)}), bf16[8,2,24,2048]{3,2,1,0:T(8,128)(2,1)S(1)}, u32[]{:S(2)}, u32[]{:S(2)}) %all-to-all-start) | async-done | bytes 1572896 | tf_op jit(solution)/shard_map/while/body/eval_jaxpr/all_to_all | solution.py:76
  120.9 4.3 gather_fusion
  127.3 5.9 collective-permute-start.7
  139.4 23.0 %scatter_fusion = bf16[16,24,2048]{2,1,0:T(8,128)(2,1)S(1)} fusion(bf16[16,24,2048]{2,1,0:T(8,128)(2,1)S(1)} %broadcast.309, s32[256]{0:T(256)S(1)} %bitcast.171, bf16[256,2048]{1,0:T(8,128)(2,1)S(1)} %broadcast_bitcast_fusion.2), kind=kCustom, calls=%fused_computation.1.clone.clone.1 | custom fusion | bytes 3147776 | tf_op jit(solution)/shard_map/while/body/eval_jaxpr/scatter | solution.py:71
  168.4 3.8 collective-permute-done
  176.7 10.2 %collective-permute-done.2 = bf16[1,1,2,24,2048]{4,3,2,1,0:T(8,128)(2,1)} collective-permute-done((bf16[1,1,2,24,2048]{4,3,2,1,0:T(8,128)(2,1)S(1)}, bf16[1,1,2,24,2048]{4,3,2,1,0:T(8,128)(2,1)}, u32[]{:S(2)}, u32[]{:S(2)}) %collective-permute-start.2) | collective-permute-done | bytes 196640 | tf_op jit(solution)/shard_map/while/body/eval_jaxpr/ppermute | solution.py:27
  188.0 5.2 fusion.80
  193.2 8.0 fusion.81
  202.5 14.4 %all-to-all-start = ((bf16[8,2,24,2048]{3,2,1,0:T(8,128)(2,1)}), bf16[8,2,24,2048]{3,2,1,0:T(8,128)(2,1)S(1)}, u32[]{:S(2)}, u32[]{:S(2)}) async-start(bf16[8,2,24,2048]{3,2,1,0:T(8,128)(2,1)} %copy.53), calls=%async_computation | async-start | bytes 3145728 | tf_op jit(solution)/shard_map/while/body/eval_jaxpr/all_to_all | solution.py:76
  217.1 36.3 %all-to-all-done = bf16[8,2,24,2048]{3,2,1,0:T(8,128)(2,1)S(1)} async-done(((bf16[8,2,24,2048]{3,2,1,0:T(8,128)(2,1)}), bf16[8,2,24,2048]{3,2,1,0:T(8,128)(2,1)S(1)}, u32[]{:S(2)}, u32[]{:S(2)}) %all-to-all-start) | async-done | bytes 1572896 | tf_op jit(solution)/shard_map/while/body/eval_jaxpr/all_to_all | solution.py:76
  253.4 4.3 gather_fusion
  259.8 4.2 collective-permute-start.7
  270.2 23.0 %scatter_fusion = bf16[16,24,2048]{2,1,0:T(8,128)(2,1)S(1)} fusion(bf16[16,24,2048]{2,1,0:T(8,128)(2,1)S(1)} %broadcast.309, s32[256]{0:T(256)S(1)} %bitcast.171, bf16[256,2048]{1,0:T(8,128)(2,1)S(1)} %broadcast_bitcast_fusion.2), kind=kCustom, calls=%fused_computation.1.clone.clone.1 | custom fusion | bytes 3147776 | tf_op jit(solution)/shard_map/while/body/eval_jaxpr/scatter | solution.py:71
  299.3 3.7 collective-permute-done
  304.0 3.5 collective-permute-start.6
  308.5 9.6 %collective-permute-done.2 = bf16[1,1,2,24,2048]{4,3,2,1,0:T(8,128)(2,1)} collective-permute-done((bf16[1,1,2,24,2048]{4,3,2,1,0:T(8,128)(2,1)S(1)}, bf16[1,1,2,24,2048]{4,3,2,1,0:T(8,128)(2,1)}, u32[]{:S(2)}, u32[]{:S(2)}) %collective-permute-start.2) | collective-permute-done | bytes 196640 | tf_op jit(solution)/shard_map/while/body/eval_jaxpr/ppermute | solution.py:27
  319.1 5.2 fusion.80
  324.3 8.0 fusion.81
  333.6 14.6 %all-to-all-start = ((bf16[8,2,24,2048]{3,2,1,0:T(8,128)(2,1)}), bf16[8,2,24,2048]{3,2,1,0:T(8,128)(2,1)S(1)}, u32[]{:S(2)}, u32[]{:S(2)}) async-start(bf16[8,2,24,2048]{3,2,1,0:T(8,128)(2,1)} %copy.53), calls=%async_computation | async-start | bytes 3145728 | tf_op jit(solution)/shard_map/while/body/eval_jaxpr/all_to_all | solution.py:76
  348.3 36.3 %all-to-all-done = bf16[8,2,24,2048]{3,2,1,0:T(8,128)(2,1)S(1)} async-done(((bf16[8,2,24,2048]{3,2,1,0:T(8,128)(2,1)}), bf16[8,2,24,2048]{3,2,1,0:T(8,128)(2,1)S(1)}, u32[]{:S(2)}, u32[]{:S(2)}) %all-to-all-start) | async-done | bytes 1572896 | tf_op jit(solution)/shard_map/while/body/eval_jaxpr/all_to_all | solution.py:76
  384.7 4.3 gather_fusion
  391.1 3.8 collective-permute-start.7
  401.1 23.0 %scatter_fusion = bf16[16,24,2048]{2,1,0:T(8,128)(2,1)S(1)} fusion(bf16[16,24,2048]{2,1,0:T(8,128)(2,1)S(1)} %broadcast.309, s32[256]{0:T(256)S(1)} %bitcast.171, bf16[256,2048]{1,0:T(8,128)(2,1)S(1)} %broadcast_bitcast_fusion.2), kind=kCustom, calls=%fused_computation.1.clone.clone.1 | custom fusion | bytes 3147776 | tf_op jit(solution)/shard_map/while/body/eval_jaxpr/scatter | solution.py:71
  430.2 3.7 collective-permute-done
  434.9 4.0 collective-permute-start.6
  439.9 9.4 %collective-permute-done.2 = bf16[1,1,2,24,2048]{4,3,2,1,0:T(8,128)(2,1)} collective-permute-done((bf16[1,1,2,24,2048]{4,3,2,1,0:T(8,128)(2,1)S(1)}, bf16[1,1,2,24,2048]{4,3,2,1,0:T(8,128)(2,1)}, u32[]{:S(2)}, u32[]{:S(2)}) %collective-permute-start.2) | collective-permute-done | bytes 196640 | tf_op jit(solution)/shard_map/while/body/eval_jaxpr/ppermute | solution.py:27
  450.4 5.2 fusion.80
  455.6 8.0 fusion.81
  464.8 14.7 %all-to-all-start = ((bf16[8,2,24,2048]{3,2,1,0:T(8,128)(2,1)}), bf16[8,2,24,2048]{3,2,1,0:T(8,128)(2,1)S(1)}, u32[]{:S(2)}, u32[]{:S(2)}) async-start(bf16[8,2,24,2048]{3,2,1,0:T(8,128)(2,1)} %copy.53), calls=%async_computation | async-start | bytes 3145728 | tf_op jit(solution)/shard_map/while/body/eval_jaxpr/all_to_all | solution.py:76
  479.7 36.3 %all-to-all-done = bf16[8,2,24,2048]{3,2,1,0:T(8,128)(2,1)S(1)} async-done(((bf16[8,2,24,2048]{3,2,1,0:T(8,128)(2,1)}), bf16[8,2,24,2048]{3,2,1,0:T(8,128)(2,1)S(1)}, u32[]{:S(2)}, u32[]{:S(2)}) %all-to-all-start) | async-done | bytes 1572896 | tf_op jit(solution)/shard_map/while/body/eval_jaxpr/all_to_all | solution.py:76
  516.0 4.3 gather_fusion
  532.0 23.0 %scatter_fusion = bf16[16,24,2048]{2,1,0:T(8,128)(2,1)S(1)} fusion(bf16[16,24,2048]{2,1,0:T(8,128)(2,1)S(1)} %broadcast.309, s32[256]{0:T(256)S(1)} %bitcast.171, bf16[256,2048]{1,0:T(8,128)(2,1)S(1)} %broadcast_bitcast_fusion.2), kind=kCustom, calls=%fused_computation.1.clone.clone.1 | custom fusion | bytes 3147776 | tf_op jit(solution)/shard_map/while/body/eval_jaxpr/scatter | solution.py:71
  561.2 3.7 collective-permute-done
  565.8 4.6 collective-permute-start.6
  571.3 9.3 %collective-permute-done.2 = bf16[1,1,2,24,2048]{4,3,2,1,0:T(8,128)(2,1)} collective-permute-done((bf16[1,1,2,24,2048]{4,3,2,1,0:T(8,128)(2,1)S(1)}, bf16[1,1,2,24,2048]{4,3,2,1,0:T(8,128)(2,1)}, u32[]{:S(2)}, u32[]{:S(2)}) %collective-permute-start.2) | collective-permute-done | bytes 196640 | tf_op jit(solution)/shard_map/while/body/eval_jaxpr/ppermute | solution.py:27
  581.7 5.2 fusion.80
  586.9 8.0 fusion.81
  596.2 14.6 %all-to-all-start = ((bf16[8,2,24,2048]{3,2,1,0:T(8,128)(2,1)}), bf16[8,2,24,2048]{3,2,1,0:T(8,128)(2,1)S(1)}, u32[]{:S(2)}, u32[]{:S(2)}) async-start(bf16[8,2,24,2048]{3,2,1,0:T(8,128)(2,1)} %copy.53), calls=%async_computation | async-start | bytes 3145728 | tf_op jit(solution)/shard_map/while/body/eval_jaxpr/all_to_all | solution.py:76
  610.9 36.3 %all-to-all-done = bf16[8,2,24,2048]{3,2,1,0:T(8,128)(2,1)S(1)} async-done(((bf16[8,2,24,2048]{3,2,1,0:T(8,128)(2,1)}), bf16[8,2,24,2048]{3,2,1,0:T(8,128)(2,1)S(1)}, u32[]{:S(2)}, u32[]{:S(2)}) %all-to-all-start) | async-done | bytes 1572896 | tf_op jit(solution)/shard_map/while/body/eval_jaxpr/all_to_all | solution.py:76
  647.2 4.3 gather_fusion
  662.9 23.0 %scatter_fusion = bf16[16,24,2048]{2,1,0:T(8,128)(2,1)S(1)} fusion(bf16[16,24,2048]{2,1,0:T(8,128)(2,1)S(1)} %broadcast.309, s32[256]{0:T(256)S(1)} %bitcast.171, bf16[256,2048]{1,0:T(8,128)(2,1)S(1)} %broadcast_bitcast_fusion.2), kind=kCustom, calls=%fused_computation.1.clone.clone.1 | custom fusion | bytes 3147776 | tf_op jit(solution)/shard_map/while/body/eval_jaxpr/scatter | solution.py:71
  692.1 3.7 collective-permute-done
  696.8 4.9 collective-permute-start.6
  702.6 9.3 %collective-permute-done.2 = bf16[1,1,2,24,2048]{4,3,2,1,0:T(8,128)(2,1)} collective-permute-done((bf16[1,1,2,24,2048]{4,3,2,1,0:T(8,128)(2,1)S(1)}, bf16[1,1,2,24,2048]{4,3,2,1,0:T(8,128)(2,1)}, u32[]{:S(2)}, u32[]{:S(2)}) %collective-permute-start.2) | collective-permute-done | bytes 196640 | tf_op jit(solution)/shard_map/while/body/eval_jaxpr/ppermute | solution.py:27
  713.0 5.2 fusion.80
  718.2 8.0 fusion.81
  727.5 14.6 %all-to-all-start = ((bf16[8,2,24,2048]{3,2,1,0:T(8,128)(2,1)}), bf16[8,2,24,2048]{3,2,1,0:T(8,128)(2,1)S(1)}, u32[]{:S(2)}, u32[]{:S(2)}) async-start(bf16[8,2,24,2048]{3,2,1,0:T(8,128)(2,1)} %copy.53), calls=%async_computation | async-start | bytes 3145728 | tf_op jit(solution)/shard_map/while/body/eval_jaxpr/all_to_all | solution.py:76
  742.2 36.3 %all-to-all-done = bf16[8,2,24,2048]{3,2,1,0:T(8,128)(2,1)S(1)} async-done(((bf16[8,2,24,2048]{3,2,1,0:T(8,128)(2,1)}), bf16[8,2,24,2048]{3,2,1,0:T(8,128)(2,1)S(1)}, u32[]{:S(2)}, u32[]{:S(2)}) %all-to-all-start) | async-done | bytes 1572896 | tf_op jit(solution)/shard_map/while/body/eval_jaxpr/all_to_all | solution.py:76
  778.5 4.3 gather_fusion
  793.9 23.0 %scatter_fusion = bf16[16,24,2048]{2,1,0:T(8,128)(2,1)S(1)} fusion(bf16[16,24,2048]{2,1,0:T(8,128)(2,1)S(1)} %broadcast.309, s32[256]{0:T(256)S(1)} %bitcast.171, bf16[256,2048]{1,0:T(8,128)(2,1)S(1)} %broadcast_bitcast_fusion.2), kind=kCustom, calls=%fused_computation.1.clone.clone.1 | custom fusion | bytes 3147776 | tf_op jit(solution)/shard_map/while/body/eval_jaxpr/scatter | solution.py:71
  823.2 3.6 collective-permute-done
  828.1 4.8 collective-permute-start.6
  833.9 9.4 %collective-permute-done.2 = bf16[1,1,2,24,2048]{4,3,2,1,0:T(8,128)(2,1)} collective-permute-done((bf16[1,1,2,24,2048]{4,3,2,1,0:T(8,128)(2,1)S(1)}, bf16[1,1,2,24,2048]{4,3,2,1,0:T(8,128)(2,1)}, u32[]{:S(2)}, u32[]{:S(2)}) %collective-permute-start.2) | collective-permute-done | bytes 196640 | tf_op jit(solution)/shard_map/while/body/eval_jaxpr/ppermute | solution.py:27
  844.3 5.2 fusion.80
  849.5 8.0 fusion.81
  858.8 14.5 %all-to-all-start = ((bf16[8,2,24,2048]{3,2,1,0:T(8,128)(2,1)}), bf16[8,2,24,2048]{3,2,1,0:T(8,128)(2,1)S(1)}, u32[]{:S(2)}, u32[]{:S(2)}) async-start(bf16[8,2,24,2048]{3,2,1,0:T(8,128)(2,1)} %copy.53), calls=%async_computation | async-start | bytes 3145728 | tf_op jit(solution)/shard_map/while/body/eval_jaxpr/all_to_all | solution.py:76
  873.4 36.2 %all-to-all-done = bf16[8,2,24,2048]{3,2,1,0:T(8,128)(2,1)S(1)} async-done(((bf16[8,2,24,2048]{3,2,1,0:T(8,128)(2,1)}), bf16[8,2,24,2048]{3,2,1,0:T(8,128)(2,1)S(1)}, u32[]{:S(2)}, u32[]{:S(2)}) %all-to-all-start) | async-done | bytes 1572896 | tf_op jit(solution)/shard_map/while/body/eval_jaxpr/all_to_all | solution.py:76
  909.7 4.3 gather_fusion
  (324 shorter events, 154.4 us)
Async XLA Ops:
  28.4 9.9 %collective-permute-start = (bf16[1,1,2,24,2048]{4,3,2,1,0:T(8,128)(2,1)S(1)}, bf16[1,1,2,24,2048]{4,3,2,1,0:T(8,128)(2,1)}, u32[]{:S(2)}, u32[]{:S(2)}) collective-permute-start(bf16[1,1,2,24,2048]{4,3,2,1,0:T(8,128)(2,1)S(1)} %get-tuple-element.527), channel_id=1, source_target_pairs={{0,1},{1,2},{2,3},{3,4},{4,5},{5,6},{6,7},{7,0},{8,9},{9,10},{10,1... | collective-permute-start | bytes 589832 | tf_op jit(solution)/shard_map/while/body/eval_jaxpr/ppermute | solution.py:27
  30.5 9.8 %collective-permute-start.1 = (bf16[1,1,2,24,2048]{4,3,2,1,0:T(8,128)(2,1)S(1)}, bf16[1,1,2,24,2048]{4,3,2,1,0:T(8,128)(2,1)}, u32[]{:S(2)}, u32[]{:S(2)}) collective-permute-start(bf16[1,1,2,24,2048]{4,3,2,1,0:T(8,128)(2,1)S(1)} %get-tuple-element.528), channel_id=1, source_target_pairs={{0,2},{1,3},{2,4},{3,5},{4,6},{5,7},{6,0},{7,1},{8,10},{9,11},{10,... | collective-permute-start | bytes 589832 | tf_op jit(solution)/shard_map/while/body/eval_jaxpr/ppermute | solution.py:27
  31.8 24.1 %collective-permute-start.2 = (bf16[1,1,2,24,2048]{4,3,2,1,0:T(8,128)(2,1)S(1)}, bf16[1,1,2,24,2048]{4,3,2,1,0:T(8,128)(2,1)}, u32[]{:S(2)}, u32[]{:S(2)}) collective-permute-start(bf16[1,1,2,24,2048]{4,3,2,1,0:T(8,128)(2,1)S(1)} %get-tuple-element.529), channel_id=1, source_target_pairs={{0,3},{1,4},{2,5},{3,6},{4,7},{5,0},{6,1},{7,2},{8,11},{9,12},{10,... | collective-permute-start | bytes 589832 | tf_op jit(solution)/shard_map/while/body/eval_jaxpr/ppermute | solution.py:27
  34.0 22.8 %collective-permute-start.3 = (bf16[1,1,2,24,2048]{4,3,2,1,0:T(8,128)(2,1)S(1)}, bf16[1,1,2,24,2048]{4,3,2,1,0:T(8,128)(2,1)S(1)}, u32[]{:S(2)}, u32[]{:S(2)}) collective-permute-start(bf16[1,1,2,24,2048]{4,3,2,1,0:T(8,128)(2,1)S(1)} %get-tuple-element.530), channel_id=1, source_target_pairs={{0,4},{1,5},{2,6},{3,7},{4,0},{5,1},{6,2},{7,3},{8,12},{9,13},{10,... | collective-permute-start | bytes 589832 | tf_op jit(solution)/shard_map/while/body/eval_jaxpr/ppermute | solution.py:27
  35.0 21.9 %collective-permute-start.4 = (bf16[1,1,2,24,2048]{4,3,2,1,0:T(8,128)(2,1)S(1)}, bf16[1,1,2,24,2048]{4,3,2,1,0:T(8,128)(2,1)S(1)}, u32[]{:S(2)}, u32[]{:S(2)}) collective-permute-start(bf16[1,1,2,24,2048]{4,3,2,1,0:T(8,128)(2,1)S(1)} %get-tuple-element.531), channel_id=1, source_target_pairs={{0,5},{1,6},{2,7},{3,0},{4,1},{5,2},{6,3},{7,4},{8,13},{9,14},{10,... | collective-permute-start | bytes 589832 | tf_op jit(solution)/shard_map/while/body/eval_jaxpr/ppermute | solution.py:27
  38.3 18.6 %collective-permute-start.5 = (bf16[1,1,2,24,2048]{4,3,2,1,0:T(8,128)(2,1)S(1)}, bf16[1,1,2,24,2048]{4,3,2,1,0:T(8,128)(2,1)S(1)}, u32[]{:S(2)}, u32[]{:S(2)}) collective-permute-start(bf16[1,1,2,24,2048]{4,3,2,1,0:T(8,128)(2,1)S(1)} %get-tuple-element.532), channel_id=1, source_target_pairs={{0,6},{1,7},{2,0},{3,1},{4,2},{5,3},{6,4},{7,5},{8,14},{9,15},{10,... | collective-permute-start | bytes 589832 | tf_op jit(solution)/shard_map/while/body/eval_jaxpr/ppermute | solution.py:27
  40.3 16.7 %collective-permute-start.6 = (bf16[1,1,2,24,2048]{4,3,2,1,0:T(8,128)(2,1)S(1)}, bf16[1,1,2,24,2048]{4,3,2,1,0:T(8,128)(2,1)S(1)}, u32[]{:S(2)}, u32[]{:S(2)}) collective-permute-start(bf16[1,1,2,24,2048]{4,3,2,1,0:T(8,128)(2,1)S(1)} %get-tuple-element.533), channel_id=1, source_target_pairs={{0,7},{1,0},{2,1},{3,2},{4,3},{5,4},{6,5},{7,6},{8,15},{9,8},{10,9... | collective-permute-start | bytes 589832 | tf_op jit(solution)/shard_map/while/body/eval_jaxpr/ppermute | solution.py:27
  71.5 49.4 %all-to-all-start = ((bf16[8,2,24,2048]{3,2,1,0:T(8,128)(2,1)}), bf16[8,2,24,2048]{3,2,1,0:T(8,128)(2,1)S(1)}, u32[]{:S(2)}, u32[]{:S(2)}) async-start(bf16[8,2,24,2048]{3,2,1,0:T(8,128)(2,1)} %copy.53), calls=%async_computation | async-start | bytes 3145728 | tf_op jit(solution)/shard_map/while/body/eval_jaxpr/all_to_all | solution.py:76
  127.3 7.8 collective-permute-start.7
  162.5 9.6 %collective-permute-start = (bf16[1,1,2,24,2048]{4,3,2,1,0:T(8,128)(2,1)S(1)}, bf16[1,1,2,24,2048]{4,3,2,1,0:T(8,128)(2,1)}, u32[]{:S(2)}, u32[]{:S(2)}) collective-permute-start(bf16[1,1,2,24,2048]{4,3,2,1,0:T(8,128)(2,1)S(1)} %get-tuple-element.527), channel_id=1, source_target_pairs={{0,1},{1,2},{2,3},{3,4},{4,5},{5,6},{6,7},{7,0},{8,9},{9,10},{10,1... | collective-permute-start | bytes 589832 | tf_op jit(solution)/shard_map/while/body/eval_jaxpr/ppermute | solution.py:27
  163.6 9.5 %collective-permute-start.1 = (bf16[1,1,2,24,2048]{4,3,2,1,0:T(8,128)(2,1)S(1)}, bf16[1,1,2,24,2048]{4,3,2,1,0:T(8,128)(2,1)}, u32[]{:S(2)}, u32[]{:S(2)}) collective-permute-start(bf16[1,1,2,24,2048]{4,3,2,1,0:T(8,128)(2,1)S(1)} %get-tuple-element.528), channel_id=1, source_target_pairs={{0,2},{1,3},{2,4},{3,5},{4,6},{5,7},{6,0},{7,1},{8,10},{9,11},{10,... | collective-permute-start | bytes 589832 | tf_op jit(solution)/shard_map/while/body/eval_jaxpr/ppermute | solution.py:27
  163.7 23.3 %collective-permute-start.2 = (bf16[1,1,2,24,2048]{4,3,2,1,0:T(8,128)(2,1)S(1)}, bf16[1,1,2,24,2048]{4,3,2,1,0:T(8,128)(2,1)}, u32[]{:S(2)}, u32[]{:S(2)}) collective-permute-start(bf16[1,1,2,24,2048]{4,3,2,1,0:T(8,128)(2,1)S(1)} %get-tuple-element.529), channel_id=1, source_target_pairs={{0,3},{1,4},{2,5},{3,6},{4,7},{5,0},{6,1},{7,2},{8,11},{9,12},{10,... | collective-permute-start | bytes 589832 | tf_op jit(solution)/shard_map/while/body/eval_jaxpr/ppermute | solution.py:27
  164.8 23.0 %collective-permute-start.3 = (bf16[1,1,2,24,2048]{4,3,2,1,0:T(8,128)(2,1)S(1)}, bf16[1,1,2,24,2048]{4,3,2,1,0:T(8,128)(2,1)S(1)}, u32[]{:S(2)}, u32[]{:S(2)}) collective-permute-start(bf16[1,1,2,24,2048]{4,3,2,1,0:T(8,128)(2,1)S(1)} %get-tuple-element.530), channel_id=1, source_target_pairs={{0,4},{1,5},{2,6},{3,7},{4,0},{5,1},{6,2},{7,3},{8,12},{9,13},{10,... | collective-permute-start | bytes 589832 | tf_op jit(solution)/shard_map/while/body/eval_jaxpr/ppermute | solution.py:27
  167.1 20.9 %collective-permute-start.4 = (bf16[1,1,2,24,2048]{4,3,2,1,0:T(8,128)(2,1)S(1)}, bf16[1,1,2,24,2048]{4,3,2,1,0:T(8,128)(2,1)S(1)}, u32[]{:S(2)}, u32[]{:S(2)}) collective-permute-start(bf16[1,1,2,24,2048]{4,3,2,1,0:T(8,128)(2,1)S(1)} %get-tuple-element.531), channel_id=1, source_target_pairs={{0,5},{1,6},{2,7},{3,0},{4,1},{5,2},{6,3},{7,4},{8,13},{9,14},{10,... | collective-permute-start | bytes 589832 | tf_op jit(solution)/shard_map/while/body/eval_jaxpr/ppermute | solution.py:27
  172.2 15.8 %collective-permute-start.5 = (bf16[1,1,2,24,2048]{4,3,2,1,0:T(8,128)(2,1)S(1)}, bf16[1,1,2,24,2048]{4,3,2,1,0:T(8,128)(2,1)S(1)}, u32[]{:S(2)}, u32[]{:S(2)}) collective-permute-start(bf16[1,1,2,24,2048]{4,3,2,1,0:T(8,128)(2,1)S(1)} %get-tuple-element.532), channel_id=1, source_target_pairs={{0,6},{1,7},{2,0},{3,1},{4,2},{5,3},{6,4},{7,5},{8,14},{9,15},{10,... | collective-permute-start | bytes 589832 | tf_op jit(solution)/shard_map/while/body/eval_jaxpr/ppermute | solution.py:27
  173.1 14.9 %collective-permute-start.6 = (bf16[1,1,2,24,2048]{4,3,2,1,0:T(8,128)(2,1)S(1)}, bf16[1,1,2,24,2048]{4,3,2,1,0:T(8,128)(2,1)S(1)}, u32[]{:S(2)}, u32[]{:S(2)}) collective-permute-start(bf16[1,1,2,24,2048]{4,3,2,1,0:T(8,128)(2,1)S(1)} %get-tuple-element.533), channel_id=1, source_target_pairs={{0,7},{1,0},{2,1},{3,2},{4,3},{5,4},{6,5},{7,6},{8,15},{9,8},{10,9... | collective-permute-start | bytes 589832 | tf_op jit(solution)/shard_map/while/body/eval_jaxpr/ppermute | solution.py:27
  202.5 50.9 %all-to-all-start = ((bf16[8,2,24,2048]{3,2,1,0:T(8,128)(2,1)}), bf16[8,2,24,2048]{3,2,1,0:T(8,128)(2,1)S(1)}, u32[]{:S(2)}, u32[]{:S(2)}) async-start(bf16[8,2,24,2048]{3,2,1,0:T(8,128)(2,1)} %copy.53), calls=%async_computation | async-start | bytes 3145728 | tf_op jit(solution)/shard_map/while/body/eval_jaxpr/all_to_all | solution.py:76
  259.8 6.1 collective-permute-start.7
  293.4 9.7 %collective-permute-start = (bf16[1,1,2,24,2048]{4,3,2,1,0:T(8,128)(2,1)S(1)}, bf16[1,1,2,24,2048]{4,3,2,1,0:T(8,128)(2,1)}, u32[]{:S(2)}, u32[]{:S(2)}) collective-permute-start(bf16[1,1,2,24,2048]{4,3,2,1,0:T(8,128)(2,1)S(1)} %get-tuple-element.527), channel_id=1, source_target_pairs={{0,1},{1,2},{2,3},{3,4},{4,5},{5,6},{6,7},{7,0},{8,9},{9,10},{10,1... | collective-permute-start | bytes 589832 | tf_op jit(solution)/shard_map/while/body/eval_jaxpr/ppermute | solution.py:27
  294.5 9.4 %collective-permute-start.1 = (bf16[1,1,2,24,2048]{4,3,2,1,0:T(8,128)(2,1)S(1)}, bf16[1,1,2,24,2048]{4,3,2,1,0:T(8,128)(2,1)}, u32[]{:S(2)}, u32[]{:S(2)}) collective-permute-start(bf16[1,1,2,24,2048]{4,3,2,1,0:T(8,128)(2,1)S(1)} %get-tuple-element.528), channel_id=1, source_target_pairs={{0,2},{1,3},{2,4},{3,5},{4,6},{5,7},{6,0},{7,1},{8,10},{9,11},{10,... | collective-permute-start | bytes 589832 | tf_op jit(solution)/shard_map/while/body/eval_jaxpr/ppermute | solution.py:27
  294.5 23.5 %collective-permute-start.2 = (bf16[1,1,2,24,2048]{4,3,2,1,0:T(8,128)(2,1)S(1)}, bf16[1,1,2,24,2048]{4,3,2,1,0:T(8,128)(2,1)}, u32[]{:S(2)}, u32[]{:S(2)}) collective-permute-start(bf16[1,1,2,24,2048]{4,3,2,1,0:T(8,128)(2,1)S(1)} %get-tuple-element.529), channel_id=1, source_target_pairs={{0,3},{1,4},{2,5},{3,6},{4,7},{5,0},{6,1},{7,2},{8,11},{9,12},{10,... | collective-permute-start | bytes 589832 | tf_op jit(solution)/shard_map/while/body/eval_jaxpr/ppermute | solution.py:27
  296.6 22.3 %collective-permute-start.3 = (bf16[1,1,2,24,2048]{4,3,2,1,0:T(8,128)(2,1)S(1)}, bf16[1,1,2,24,2048]{4,3,2,1,0:T(8,128)(2,1)S(1)}, u32[]{:S(2)}, u32[]{:S(2)}) collective-permute-start(bf16[1,1,2,24,2048]{4,3,2,1,0:T(8,128)(2,1)S(1)} %get-tuple-element.530), channel_id=1, source_target_pairs={{0,4},{1,5},{2,6},{3,7},{4,0},{5,1},{6,2},{7,3},{8,12},{9,13},{10,... | collective-permute-start | bytes 589832 | tf_op jit(solution)/shard_map/while/body/eval_jaxpr/ppermute | solution.py:27
  297.9 21.1 %collective-permute-start.4 = (bf16[1,1,2,24,2048]{4,3,2,1,0:T(8,128)(2,1)S(1)}, bf16[1,1,2,24,2048]{4,3,2,1,0:T(8,128)(2,1)S(1)}, u32[]{:S(2)}, u32[]{:S(2)}) collective-permute-start(bf16[1,1,2,24,2048]{4,3,2,1,0:T(8,128)(2,1)S(1)} %get-tuple-element.531), channel_id=1, source_target_pairs={{0,5},{1,6},{2,7},{3,0},{4,1},{5,2},{6,3},{7,4},{8,13},{9,14},{10,... | collective-permute-start | bytes 589832 | tf_op jit(solution)/shard_map/while/body/eval_jaxpr/ppermute | solution.py:27
  303.0 16.0 %collective-permute-start.5 = (bf16[1,1,2,24,2048]{4,3,2,1,0:T(8,128)(2,1)S(1)}, bf16[1,1,2,24,2048]{4,3,2,1,0:T(8,128)(2,1)S(1)}, u32[]{:S(2)}, u32[]{:S(2)}) collective-permute-start(bf16[1,1,2,24,2048]{4,3,2,1,0:T(8,128)(2,1)S(1)} %get-tuple-element.532), channel_id=1, source_target_pairs={{0,6},{1,7},{2,0},{3,1},{4,2},{5,3},{6,4},{7,5},{8,14},{9,15},{10,... | collective-permute-start | bytes 589832 | tf_op jit(solution)/shard_map/while/body/eval_jaxpr/ppermute | solution.py:27
  304.0 15.1 %collective-permute-start.6 = (bf16[1,1,2,24,2048]{4,3,2,1,0:T(8,128)(2,1)S(1)}, bf16[1,1,2,24,2048]{4,3,2,1,0:T(8,128)(2,1)S(1)}, u32[]{:S(2)}, u32[]{:S(2)}) collective-permute-start(bf16[1,1,2,24,2048]{4,3,2,1,0:T(8,128)(2,1)S(1)} %get-tuple-element.533), channel_id=1, source_target_pairs={{0,7},{1,0},{2,1},{3,2},{4,3},{5,4},{6,5},{7,6},{8,15},{9,8},{10,9... | collective-permute-start | bytes 589832 | tf_op jit(solution)/shard_map/while/body/eval_jaxpr/ppermute | solution.py:27
  333.6 51.1 %all-to-all-start = ((bf16[8,2,24,2048]{3,2,1,0:T(8,128)(2,1)}), bf16[8,2,24,2048]{3,2,1,0:T(8,128)(2,1)S(1)}, u32[]{:S(2)}, u32[]{:S(2)}) async-start(bf16[8,2,24,2048]{3,2,1,0:T(8,128)(2,1)} %copy.53), calls=%async_computation | async-start | bytes 3145728 | tf_op jit(solution)/shard_map/while/body/eval_jaxpr/all_to_all | solution.py:76
  391.1 5.7 collective-permute-start.7
  424.3 9.7 %collective-permute-start = (bf16[1,1,2,24,2048]{4,3,2,1,0:T(8,128)(2,1)S(1)}, bf16[1,1,2,24,2048]{4,3,2,1,0:T(8,128)(2,1)}, u32[]{:S(2)}, u32[]{:S(2)}) collective-permute-start(bf16[1,1,2,24,2048]{4,3,2,1,0:T(8,128)(2,1)S(1)} %get-tuple-element.527), channel_id=1, source_target_pairs={{0,1},{1,2},{2,3},{3,4},{4,5},{5,6},{6,7},{7,0},{8,9},{9,10},{10,1... | collective-permute-start | bytes 589832 | tf_op jit(solution)/shard_map/while/body/eval_jaxpr/ppermute | solution.py:27
  425.5 9.4 %collective-permute-start.1 = (bf16[1,1,2,24,2048]{4,3,2,1,0:T(8,128)(2,1)S(1)}, bf16[1,1,2,24,2048]{4,3,2,1,0:T(8,128)(2,1)}, u32[]{:S(2)}, u32[]{:S(2)}) collective-permute-start(bf16[1,1,2,24,2048]{4,3,2,1,0:T(8,128)(2,1)S(1)} %get-tuple-element.528), channel_id=1, source_target_pairs={{0,2},{1,3},{2,4},{3,5},{4,6},{5,7},{6,0},{7,1},{8,10},{9,11},{10,... | collective-permute-start | bytes 589832 | tf_op jit(solution)/shard_map/while/body/eval_jaxpr/ppermute | solution.py:27
  425.5 23.8 %collective-permute-start.2 = (bf16[1,1,2,24,2048]{4,3,2,1,0:T(8,128)(2,1)S(1)}, bf16[1,1,2,24,2048]{4,3,2,1,0:T(8,128)(2,1)}, u32[]{:S(2)}, u32[]{:S(2)}) collective-permute-start(bf16[1,1,2,24,2048]{4,3,2,1,0:T(8,128)(2,1)S(1)} %get-tuple-element.529), channel_id=1, source_target_pairs={{0,3},{1,4},{2,5},{3,6},{4,7},{5,0},{6,1},{7,2},{8,11},{9,12},{10,... | collective-permute-start | bytes 589832 | tf_op jit(solution)/shard_map/while/body/eval_jaxpr/ppermute | solution.py:27
  427.7 22.6 %collective-permute-start.3 = (bf16[1,1,2,24,2048]{4,3,2,1,0:T(8,128)(2,1)S(1)}, bf16[1,1,2,24,2048]{4,3,2,1,0:T(8,128)(2,1)S(1)}, u32[]{:S(2)}, u32[]{:S(2)}) collective-permute-start(bf16[1,1,2,24,2048]{4,3,2,1,0:T(8,128)(2,1)S(1)} %get-tuple-element.530), channel_id=1, source_target_pairs={{0,4},{1,5},{2,6},{3,7},{4,0},{5,1},{6,2},{7,3},{8,12},{9,13},{10,... | collective-permute-start | bytes 589832 | tf_op jit(solution)/shard_map/while/body/eval_jaxpr/ppermute | solution.py:27
  428.8 21.5 %collective-permute-start.4 = (bf16[1,1,2,24,2048]{4,3,2,1,0:T(8,128)(2,1)S(1)}, bf16[1,1,2,24,2048]{4,3,2,1,0:T(8,128)(2,1)S(1)}, u32[]{:S(2)}, u32[]{:S(2)}) collective-permute-start(bf16[1,1,2,24,2048]{4,3,2,1,0:T(8,128)(2,1)S(1)} %get-tuple-element.531), channel_id=1, source_target_pairs={{0,5},{1,6},{2,7},{3,0},{4,1},{5,2},{6,3},{7,4},{8,13},{9,14},{10,... | collective-permute-start | bytes 589832 | tf_op jit(solution)/shard_map/while/body/eval_jaxpr/ppermute | solution.py:27
  433.9 16.4 %collective-permute-start.5 = (bf16[1,1,2,24,2048]{4,3,2,1,0:T(8,128)(2,1)S(1)}, bf16[1,1,2,24,2048]{4,3,2,1,0:T(8,128)(2,1)S(1)}, u32[]{:S(2)}, u32[]{:S(2)}) collective-permute-start(bf16[1,1,2,24,2048]{4,3,2,1,0:T(8,128)(2,1)S(1)} %get-tuple-element.532), channel_id=1, source_target_pairs={{0,6},{1,7},{2,0},{3,1},{4,2},{5,3},{6,4},{7,5},{8,14},{9,15},{10,... | collective-permute-start | bytes 589832 | tf_op jit(solution)/shard_map/while/body/eval_jaxpr/ppermute | solution.py:27
  434.9 15.5 %collective-permute-start.6 = (bf16[1,1,2,24,2048]{4,3,2,1,0:T(8,128)(2,1)S(1)}, bf16[1,1,2,24,2048]{4,3,2,1,0:T(8,128)(2,1)S(1)}, u32[]{:S(2)}, u32[]{:S(2)}) collective-permute-start(bf16[1,1,2,24,2048]{4,3,2,1,0:T(8,128)(2,1)S(1)} %get-tuple-element.533), channel_id=1, source_target_pairs={{0,7},{1,0},{2,1},{3,2},{4,3},{5,4},{6,5},{7,6},{8,15},{9,8},{10,9... | collective-permute-start | bytes 589832 | tf_op jit(solution)/shard_map/while/body/eval_jaxpr/ppermute | solution.py:27
  464.8 14.7 %copy-start = (f32[1,4,32,8]{2,3,1,0:T(8,128)S(1)}, f32[1,4,32,8]{2,3,1,0:T(8,128)}, u32[]{:S(2)}) copy-start(f32[1,4,32,8]{2,3,1,0:T(8,128)} %get-tuple-element.605) | copy-start | bytes 12292 | tf_op jit(solution)/shard_map/while
  464.8 51.1 %all-to-all-start = ((bf16[8,2,24,2048]{3,2,1,0:T(8,128)(2,1)}), bf16[8,2,24,2048]{3,2,1,0:T(8,128)(2,1)S(1)}, u32[]{:S(2)}, u32[]{:S(2)}) async-start(bf16[8,2,24,2048]{3,2,1,0:T(8,128)(2,1)} %copy.53), calls=%async_computation | async-start | bytes 3145728 | tf_op jit(solution)/shard_map/while/body/eval_jaxpr/all_to_all | solution.py:76
  522.4 5.4 collective-permute-start.7
  555.2 9.7 %collective-permute-start = (bf16[1,1,2,24,2048]{4,3,2,1,0:T(8,128)(2,1)S(1)}, bf16[1,1,2,24,2048]{4,3,2,1,0:T(8,128)(2,1)}, u32[]{:S(2)}, u32[]{:S(2)}) collective-permute-start(bf16[1,1,2,24,2048]{4,3,2,1,0:T(8,128)(2,1)S(1)} %get-tuple-element.527), channel_id=1, source_target_pairs={{0,1},{1,2},{2,3},{3,4},{4,5},{5,6},{6,7},{7,0},{8,9},{9,10},{10,1... | collective-permute-start | bytes 589832 | tf_op jit(solution)/shard_map/while/body/eval_jaxpr/ppermute | solution.py:27
  556.4 9.4 %collective-permute-start.1 = (bf16[1,1,2,24,2048]{4,3,2,1,0:T(8,128)(2,1)S(1)}, bf16[1,1,2,24,2048]{4,3,2,1,0:T(8,128)(2,1)}, u32[]{:S(2)}, u32[]{:S(2)}) collective-permute-start(bf16[1,1,2,24,2048]{4,3,2,1,0:T(8,128)(2,1)S(1)} %get-tuple-element.528), channel_id=1, source_target_pairs={{0,2},{1,3},{2,4},{3,5},{4,6},{5,7},{6,0},{7,1},{8,10},{9,11},{10,... | collective-permute-start | bytes 589832 | tf_op jit(solution)/shard_map/while/body/eval_jaxpr/ppermute | solution.py:27
  556.4 24.2 %collective-permute-start.2 = (bf16[1,1,2,24,2048]{4,3,2,1,0:T(8,128)(2,1)S(1)}, bf16[1,1,2,24,2048]{4,3,2,1,0:T(8,128)(2,1)}, u32[]{:S(2)}, u32[]{:S(2)}) collective-permute-start(bf16[1,1,2,24,2048]{4,3,2,1,0:T(8,128)(2,1)S(1)} %get-tuple-element.529), channel_id=1, source_target_pairs={{0,3},{1,4},{2,5},{3,6},{4,7},{5,0},{6,1},{7,2},{8,11},{9,12},{10,... | collective-permute-start | bytes 589832 | tf_op jit(solution)/shard_map/while/body/eval_jaxpr/ppermute | solution.py:27
  558.7 22.9 %collective-permute-start.3 = (bf16[1,1,2,24,2048]{4,3,2,1,0:T(8,128)(2,1)S(1)}, bf16[1,1,2,24,2048]{4,3,2,1,0:T(8,128)(2,1)S(1)}, u32[]{:S(2)}, u32[]{:S(2)}) collective-permute-start(bf16[1,1,2,24,2048]{4,3,2,1,0:T(8,128)(2,1)S(1)} %get-tuple-element.530), channel_id=1, source_target_pairs={{0,4},{1,5},{2,6},{3,7},{4,0},{5,1},{6,2},{7,3},{8,12},{9,13},{10,... | collective-permute-start | bytes 589832 | tf_op jit(solution)/shard_map/while/body/eval_jaxpr/ppermute | solution.py:27
  559.7 21.9 %collective-permute-start.4 = (bf16[1,1,2,24,2048]{4,3,2,1,0:T(8,128)(2,1)S(1)}, bf16[1,1,2,24,2048]{4,3,2,1,0:T(8,128)(2,1)S(1)}, u32[]{:S(2)}, u32[]{:S(2)}) collective-permute-start(bf16[1,1,2,24,2048]{4,3,2,1,0:T(8,128)(2,1)S(1)} %get-tuple-element.531), channel_id=1, source_target_pairs={{0,5},{1,6},{2,7},{3,0},{4,1},{5,2},{6,3},{7,4},{8,13},{9,14},{10,... | collective-permute-start | bytes 589832 | tf_op jit(solution)/shard_map/while/body/eval_jaxpr/ppermute | solution.py:27
  564.9 16.8 %collective-permute-start.5 = (bf16[1,1,2,24,2048]{4,3,2,1,0:T(8,128)(2,1)S(1)}, bf16[1,1,2,24,2048]{4,3,2,1,0:T(8,128)(2,1)S(1)}, u32[]{:S(2)}, u32[]{:S(2)}) collective-permute-start(bf16[1,1,2,24,2048]{4,3,2,1,0:T(8,128)(2,1)S(1)} %get-tuple-element.532), channel_id=1, source_target_pairs={{0,6},{1,7},{2,0},{3,1},{4,2},{5,3},{6,4},{7,5},{8,14},{9,15},{10,... | collective-permute-start | bytes 589832 | tf_op jit(solution)/shard_map/while/body/eval_jaxpr/ppermute | solution.py:27
  565.8 15.9 %collective-permute-start.6 = (bf16[1,1,2,24,2048]{4,3,2,1,0:T(8,128)(2,1)S(1)}, bf16[1,1,2,24,2048]{4,3,2,1,0:T(8,128)(2,1)S(1)}, u32[]{:S(2)}, u32[]{:S(2)}) collective-permute-start(bf16[1,1,2,24,2048]{4,3,2,1,0:T(8,128)(2,1)S(1)} %get-tuple-element.533), channel_id=1, source_target_pairs={{0,7},{1,0},{2,1},{3,2},{4,3},{5,4},{6,5},{7,6},{8,15},{9,8},{10,9... | collective-permute-start | bytes 589832 | tf_op jit(solution)/shard_map/while/body/eval_jaxpr/ppermute | solution.py:27
  596.2 51.1 %all-to-all-start = ((bf16[8,2,24,2048]{3,2,1,0:T(8,128)(2,1)}), bf16[8,2,24,2048]{3,2,1,0:T(8,128)(2,1)S(1)}, u32[]{:S(2)}, u32[]{:S(2)}) async-start(bf16[8,2,24,2048]{3,2,1,0:T(8,128)(2,1)} %copy.53), calls=%async_computation | async-start | bytes 3145728 | tf_op jit(solution)/shard_map/while/body/eval_jaxpr/all_to_all | solution.py:76
  653.7 5.0 collective-permute-start.7
  686.1 9.7 %collective-permute-start = (bf16[1,1,2,24,2048]{4,3,2,1,0:T(8,128)(2,1)S(1)}, bf16[1,1,2,24,2048]{4,3,2,1,0:T(8,128)(2,1)}, u32[]{:S(2)}, u32[]{:S(2)}) collective-permute-start(bf16[1,1,2,24,2048]{4,3,2,1,0:T(8,128)(2,1)S(1)} %get-tuple-element.527), channel_id=1, source_target_pairs={{0,1},{1,2},{2,3},{3,4},{4,5},{5,6},{6,7},{7,0},{8,9},{9,10},{10,1... | collective-permute-start | bytes 589832 | tf_op jit(solution)/shard_map/while/body/eval_jaxpr/ppermute | solution.py:27
  687.4 9.4 %collective-permute-start.1 = (bf16[1,1,2,24,2048]{4,3,2,1,0:T(8,128)(2,1)S(1)}, bf16[1,1,2,24,2048]{4,3,2,1,0:T(8,128)(2,1)}, u32[]{:S(2)}, u32[]{:S(2)}) collective-permute-start(bf16[1,1,2,24,2048]{4,3,2,1,0:T(8,128)(2,1)S(1)} %get-tuple-element.528), channel_id=1, source_target_pairs={{0,2},{1,3},{2,4},{3,5},{4,6},{5,7},{6,0},{7,1},{8,10},{9,11},{10,... | collective-permute-start | bytes 589832 | tf_op jit(solution)/shard_map/while/body/eval_jaxpr/ppermute | solution.py:27
  687.4 24.6 %collective-permute-start.2 = (bf16[1,1,2,24,2048]{4,3,2,1,0:T(8,128)(2,1)S(1)}, bf16[1,1,2,24,2048]{4,3,2,1,0:T(8,128)(2,1)}, u32[]{:S(2)}, u32[]{:S(2)}) collective-permute-start(bf16[1,1,2,24,2048]{4,3,2,1,0:T(8,128)(2,1)S(1)} %get-tuple-element.529), channel_id=1, source_target_pairs={{0,3},{1,4},{2,5},{3,6},{4,7},{5,0},{6,1},{7,2},{8,11},{9,12},{10,... | collective-permute-start | bytes 589832 | tf_op jit(solution)/shard_map/while/body/eval_jaxpr/ppermute | solution.py:27
  689.6 23.3 %collective-permute-start.3 = (bf16[1,1,2,24,2048]{4,3,2,1,0:T(8,128)(2,1)S(1)}, bf16[1,1,2,24,2048]{4,3,2,1,0:T(8,128)(2,1)S(1)}, u32[]{:S(2)}, u32[]{:S(2)}) collective-permute-start(bf16[1,1,2,24,2048]{4,3,2,1,0:T(8,128)(2,1)S(1)} %get-tuple-element.530), channel_id=1, source_target_pairs={{0,4},{1,5},{2,6},{3,7},{4,0},{5,1},{6,2},{7,3},{8,12},{9,13},{10,... | collective-permute-start | bytes 589832 | tf_op jit(solution)/shard_map/while/body/eval_jaxpr/ppermute | solution.py:27
  690.7 22.2 %collective-permute-start.4 = (bf16[1,1,2,24,2048]{4,3,2,1,0:T(8,128)(2,1)S(1)}, bf16[1,1,2,24,2048]{4,3,2,1,0:T(8,128)(2,1)S(1)}, u32[]{:S(2)}, u32[]{:S(2)}) collective-permute-start(bf16[1,1,2,24,2048]{4,3,2,1,0:T(8,128)(2,1)S(1)} %get-tuple-element.531), channel_id=1, source_target_pairs={{0,5},{1,6},{2,7},{3,0},{4,1},{5,2},{6,3},{7,4},{8,13},{9,14},{10,... | collective-permute-start | bytes 589832 | tf_op jit(solution)/shard_map/while/body/eval_jaxpr/ppermute | solution.py:27
  695.8 17.2 %collective-permute-start.5 = (bf16[1,1,2,24,2048]{4,3,2,1,0:T(8,128)(2,1)S(1)}, bf16[1,1,2,24,2048]{4,3,2,1,0:T(8,128)(2,1)S(1)}, u32[]{:S(2)}, u32[]{:S(2)}) collective-permute-start(bf16[1,1,2,24,2048]{4,3,2,1,0:T(8,128)(2,1)S(1)} %get-tuple-element.532), channel_id=1, source_target_pairs={{0,6},{1,7},{2,0},{3,1},{4,2},{5,3},{6,4},{7,5},{8,14},{9,15},{10,... | collective-permute-start | bytes 589832 | tf_op jit(solution)/shard_map/while/body/eval_jaxpr/ppermute | solution.py:27
  696.8 16.2 %collective-permute-start.6 = (bf16[1,1,2,24,2048]{4,3,2,1,0:T(8,128)(2,1)S(1)}, bf16[1,1,2,24,2048]{4,3,2,1,0:T(8,128)(2,1)S(1)}, u32[]{:S(2)}, u32[]{:S(2)}) collective-permute-start(bf16[1,1,2,24,2048]{4,3,2,1,0:T(8,128)(2,1)S(1)} %get-tuple-element.533), channel_id=1, source_target_pairs={{0,7},{1,0},{2,1},{3,2},{4,3},{5,4},{6,5},{7,6},{8,15},{9,8},{10,9... | collective-permute-start | bytes 589832 | tf_op jit(solution)/shard_map/while/body/eval_jaxpr/ppermute | solution.py:27
  727.5 51.0 %all-to-all-start = ((bf16[8,2,24,2048]{3,2,1,0:T(8,128)(2,1)}), bf16[8,2,24,2048]{3,2,1,0:T(8,128)(2,1)S(1)}, u32[]{:S(2)}, u32[]{:S(2)}) async-start(bf16[8,2,24,2048]{3,2,1,0:T(8,128)(2,1)} %copy.53), calls=%async_computation | async-start | bytes 3145728 | tf_op jit(solution)/shard_map/while/body/eval_jaxpr/all_to_all | solution.py:76
  784.9 4.8 collective-permute-start.7
  817.1 9.7 %collective-permute-start = (bf16[1,1,2,24,2048]{4,3,2,1,0:T(8,128)(2,1)S(1)}, bf16[1,1,2,24,2048]{4,3,2,1,0:T(8,128)(2,1)}, u32[]{:S(2)}, u32[]{:S(2)}) collective-permute-start(bf16[1,1,2,24,2048]{4,3,2,1,0:T(8,128)(2,1)S(1)} %get-tuple-element.527), channel_id=1, source_target_pairs={{0,1},{1,2},{2,3},{3,4},{4,5},{5,6},{6,7},{7,0},{8,9},{9,10},{10,1... | collective-permute-start | bytes 589832 | tf_op jit(solution)/shard_map/while/body/eval_jaxpr/ppermute | solution.py:27
  818.3 9.8 %collective-permute-start.1 = (bf16[1,1,2,24,2048]{4,3,2,1,0:T(8,128)(2,1)S(1)}, bf16[1,1,2,24,2048]{4,3,2,1,0:T(8,128)(2,1)}, u32[]{:S(2)}, u32[]{:S(2)}) collective-permute-start(bf16[1,1,2,24,2048]{4,3,2,1,0:T(8,128)(2,1)S(1)} %get-tuple-element.528), channel_id=1, source_target_pairs={{0,2},{1,3},{2,4},{3,5},{4,6},{5,7},{6,0},{7,1},{8,10},{9,11},{10,... | collective-permute-start | bytes 589832 | tf_op jit(solution)/shard_map/while/body/eval_jaxpr/ppermute | solution.py:27
  818.3 24.9 %collective-permute-start.2 = (bf16[1,1,2,24,2048]{4,3,2,1,0:T(8,128)(2,1)S(1)}, bf16[1,1,2,24,2048]{4,3,2,1,0:T(8,128)(2,1)}, u32[]{:S(2)}, u32[]{:S(2)}) collective-permute-start(bf16[1,1,2,24,2048]{4,3,2,1,0:T(8,128)(2,1)S(1)} %get-tuple-element.529), channel_id=1, source_target_pairs={{0,3},{1,4},{2,5},{3,6},{4,7},{5,0},{6,1},{7,2},{8,11},{9,12},{10,... | collective-permute-start | bytes 589832 | tf_op jit(solution)/shard_map/while/body/eval_jaxpr/ppermute | solution.py:27
  820.7 23.5 %collective-permute-start.3 = (bf16[1,1,2,24,2048]{4,3,2,1,0:T(8,128)(2,1)S(1)}, bf16[1,1,2,24,2048]{4,3,2,1,0:T(8,128)(2,1)S(1)}, u32[]{:S(2)}, u32[]{:S(2)}) collective-permute-start(bf16[1,1,2,24,2048]{4,3,2,1,0:T(8,128)(2,1)S(1)} %get-tuple-element.530), channel_id=1, source_target_pairs={{0,4},{1,5},{2,6},{3,7},{4,0},{5,1},{6,2},{7,3},{8,12},{9,13},{10,... | collective-permute-start | bytes 589832 | tf_op jit(solution)/shard_map/while/body/eval_jaxpr/ppermute | solution.py:27
  821.6 22.6 %collective-permute-start.4 = (bf16[1,1,2,24,2048]{4,3,2,1,0:T(8,128)(2,1)S(1)}, bf16[1,1,2,24,2048]{4,3,2,1,0:T(8,128)(2,1)S(1)}, u32[]{:S(2)}, u32[]{:S(2)}) collective-permute-start(bf16[1,1,2,24,2048]{4,3,2,1,0:T(8,128)(2,1)S(1)} %get-tuple-element.531), channel_id=1, source_target_pairs={{0,5},{1,6},{2,7},{3,0},{4,1},{5,2},{6,3},{7,4},{8,13},{9,14},{10,... | collective-permute-start | bytes 589832 | tf_op jit(solution)/shard_map/while/body/eval_jaxpr/ppermute | solution.py:27
  826.8 17.5 %collective-permute-start.5 = (bf16[1,1,2,24,2048]{4,3,2,1,0:T(8,128)(2,1)S(1)}, bf16[1,1,2,24,2048]{4,3,2,1,0:T(8,128)(2,1)S(1)}, u32[]{:S(2)}, u32[]{:S(2)}) collective-permute-start(bf16[1,1,2,24,2048]{4,3,2,1,0:T(8,128)(2,1)S(1)} %get-tuple-element.532), channel_id=1, source_target_pairs={{0,6},{1,7},{2,0},{3,1},{4,2},{5,3},{6,4},{7,5},{8,14},{9,15},{10,... | collective-permute-start | bytes 589832 | tf_op jit(solution)/shard_map/while/body/eval_jaxpr/ppermute | solution.py:27
  828.1 16.2 %collective-permute-start.6 = (bf16[1,1,2,24,2048]{4,3,2,1,0:T(8,128)(2,1)S(1)}, bf16[1,1,2,24,2048]{4,3,2,1,0:T(8,128)(2,1)S(1)}, u32[]{:S(2)}, u32[]{:S(2)}) collective-permute-start(bf16[1,1,2,24,2048]{4,3,2,1,0:T(8,128)(2,1)S(1)} %get-tuple-element.533), channel_id=1, source_target_pairs={{0,7},{1,0},{2,1},{3,2},{4,3},{5,4},{6,5},{7,6},{8,15},{9,8},{10,9... | collective-permute-start | bytes 589832 | tf_op jit(solution)/shard_map/while/body/eval_jaxpr/ppermute | solution.py:27
  858.8 50.9 %all-to-all-start = ((bf16[8,2,24,2048]{3,2,1,0:T(8,128)(2,1)}), bf16[8,2,24,2048]{3,2,1,0:T(8,128)(2,1)S(1)}, u32[]{:S(2)}, u32[]{:S(2)}) async-start(bf16[8,2,24,2048]{3,2,1,0:T(8,128)(2,1)} %copy.53), calls=%async_computation | async-start | bytes 3145728 | tf_op jit(solution)/shard_map/while/body/eval_jaxpr/all_to_all | solution.py:76
  916.1 4.5 collective-permute-start.7
  (6 other events, 87.1 us)
